TPU v7x, 32 devices: a whole 2x2x4 slice. The times are simulated.
32 devices in a mesh: dom: 16 (over z, y, x), grp: 2 (over core).
Axes of the slice: x: 2, y: 2, z: 4, core: 2. Of those that a mesh axis runs over, the one named last changes fastest.
Arguments:
- tangent_tiles: bfloat16 [4096, 128, 128], P(('grp', 'dom')), parts along dimension 0, may hold values from -0.5 to 0.5
- tile_blocks: int32 [2048, 2], P('dom'), may hold values from 0 to 127, as said below
- block_home: int32 [128], replicated, may hold values from 0 to 127, as said below
- tile_count: int32 [16], P('dom'), may hold values from 48 to 128, as said below
- basis: bfloat16 [16384, 256], P('dom'), may hold values from -0.29882812 to 0.29882812
Outputs:
- reduced: float32 [512, 256], P('grp'), parts along dimension 0
There are 2 independent parts, one for each index of `grp`. A program takes and returns all parts, laid end to end along the dimension named above; an argument that names none is the same for every part. Nothing has to cross between parts.
Inputs may be any that keep to these rules, and one draw needn't show every extreme that they name: `tile_blocks`: every row block named by a device's tile slots has its position held by one of the devices with dom index from that device's index - 4 to its index + 8 // 2 - 1, taken cyclically. Among the row blocks named by one device's 128 slots, at most 2 distinct ones have their position held by any one device; every device reaches 2 for some holder. `block_home`: A permutation of the row blocks. `tile_count`: some device has exactly 128 live slots.
All inputs are finite; a program needn't handle non-finite values.
Results may differ from a plain program's by a relative error of at most 0.0029.
Values may be sent and summed in bfloat16 or wider, within the bound.
A program may use at most 64 MiB of HBM per device.

v0:
```python
import jax
import jax.numpy as jnp
from jax import lax
from jax.sharding import PartitionSpec as P

CAP = 2
NEAR = 8
GROUP = 16


def shifted(value, axis, steps):
    count = lax.axis_size(axis)
    pairs = [(source, (source + steps) % count) for source in range(count)]
    return lax.ppermute(value, axis, pairs)


def on_device(tangent_tiles, tile_blocks, block_home, tile_count, basis):
    ndom = lax.axis_size("dom")
    tile_dev = tangent_tiles.shape[0]
    block = tangent_tiles.shape[1]
    rank = basis.shape[1]
    blk_dev = basis.shape[0] // block
    stored = basis.reshape(blk_dev, block, rank)
    place = jnp.take(block_home, tile_blocks.reshape(-1), axis=0)
    places = jnp.arange(ndom * blk_dev, dtype=jnp.int32)
    wanted = jnp.any(place[:, None] == places[None, :], axis=0).astype(jnp.int32)
    wanted = wanted.reshape(ndom, blk_dev)
    order = jnp.cumsum(wanted, axis=1) - 1
    levels = jnp.arange(CAP, dtype=jnp.int32)
    chosen = (wanted[:, :, None] == 1) & (order[:, :, None] == levels[None, None, :])
    local_ids = jnp.arange(blk_dev, dtype=jnp.int32)[None, :, None]
    requests = jnp.sum(jnp.where(chosen, local_ids, 0), axis=1)
    holder = place // blk_dev
    flat_order = order.reshape(-1)
    level_of = jnp.take(flat_order, place, axis=0)
    myself = lax.axis_index("dom")
    pieces = []
    for step_k in range(NEAR):
        away = step_k - NEAR // 2
        target = (myself + away) % ndom
        asking = lax.dynamic_index_in_dim(requests, target, 0, keepdims=False)
        if away == 0:
            pieces.append(jnp.take(stored, asking, axis=0))
        else:
            asked = shifted(asking, "dom", away)
            served = jnp.take(stored, asked, axis=0)
            pieces.append(shifted(served, "dom", -away))
    fetched = jnp.concatenate(pieces, axis=0)
    window_pos = (holder - myself + NEAR // 2) % ndom
    slot_of = window_pos * CAP + level_of
    slot_of = slot_of.reshape(tile_dev, 2)
    live = (jnp.arange(tile_dev, dtype=jnp.int32) < tile_count[0]).astype(jnp.float32)

    def project(step, total):
        begin = step * GROUP
        tile_set = lax.dynamic_slice_in_dim(tangent_tiles, begin, GROUP, 0)
        link_set = lax.dynamic_slice_in_dim(slot_of, begin, GROUP, 0)
        live_set = lax.dynamic_slice_in_dim(live, begin, GROUP, 0)
        cols = jnp.take(fetched, link_set[:, 1], axis=0)
        rows = jnp.take(fetched, link_set[:, 0], axis=0)
        right = jnp.einsum("tab,tbr->tar", tile_set, cols, preferred_element_type=jnp.float32)
        right = (right * live_set[:, None, None]).astype(jnp.bfloat16)
        return total + jnp.einsum(
            "ar,as->rs",
            rows.reshape(GROUP * block, rank),
            right.reshape(GROUP * block, rank),
            preferred_element_type=jnp.float32,
        )

    partial_sum = lax.fori_loop(0, tile_dev // GROUP, project, jnp.zeros((rank, rank), jnp.float32))
    reduced = lax.psum(partial_sum, "dom")
    return reduced


def solution(mesh):
    return jax.shard_map(
        on_device,
        mesh=mesh,
        in_specs=(P(("grp", "dom"), None, None), P("dom", None), P(), P("dom"), P("dom", None)),
        out_specs=P("grp", None),
        check_vma=False,
    )
```

profile of v0, /device:TPU:0, one launch (start us, length us, event | category | flops | bytes accessed | tf_op | source)
XLA Modules:
  0.0 211.4 jit_solution(7998382532682025767)
XLA Ops:
  6.5 0.8 copy.16
  7.4 0.1 reshape.52
  7.5 1.9 gather_fusion.2
  9.5 0.1 fusion.18
  9.7 0.2 reduce_window_sum.11
  10.0 0.3 fusion.29
  10.3 4.0 %collective-permute-start.12 = (s32[2]{0:T(128)S(1)}, s32[2]{0:T(128)S(1)}, u32[]{:S(2)}, u32[]{:S(2)}) collective-permute-start(s32[2]{0:T(128)S(1)} %get-tuple-element.157), channel_id=1, source_target_pairs={{0,6},{2,8},{4,10},{6,12},{8,14},{10,16},{12,18},{14,20},{16,22},{... | collective-permute-start | bytes 32 | tf_op jit(solution)/shard_map/ppermute | solution.py:14
  14.3 1.5 collective-permute-start.10
  15.8 0.6 collective-permute-start.8
  16.4 5.0 %collective-permute-start.6 = (s32[2]{0:T(128)S(1)}, s32[2]{0:T(128)S(1)}, u32[]{:S(2)}, u32[]{:S(2)}) collective-permute-start(s32[2]{0:T(128)S(1)} %get-tuple-element.161), channel_id=1, source_target_pairs={{0,30},{2,0},{4,2},{6,4},{8,6},{10,8},{12,10},{14,12},{16,14},{18,... | collective-permute-start | bytes 32 | tf_op jit(solution)/shard_map/ppermute | solution.py:14
  21.5 0.5 collective-permute-start.4
  22.0 0.1 sub.22
  22.8 1.9 gather_fusion.3
  24.7 0.1 reshape.53
  24.9 0.6 gather_fusion.8
  25.5 0.4 collective-permute-start.2
  25.9 1.5 collective-permute-start
  27.5 2.5 %collective-permute-done.2 = s32[2]{0:T(128)S(1)} collective-permute-done((s32[2]{0:T(128)S(1)}, s32[2]{0:T(128)S(1)}, u32[]{:S(2)}, u32[]{:S(2)}) %collective-permute-start.2) | collective-permute-done | bytes 40 | tf_op jit(solution)/shard_map/ppermute | solution.py:14
  30.0 0.6 gather_fusion.4
  30.6 0.6 gather_fusion.5
  31.2 0.6 gather_fusion.6
  31.7 0.6 gather_fusion.7
  32.3 0.6 gather_fusion.9
  32.9 0.6 gather_fusion.10
  33.4 0.6 gather_fusion.11
  34.1 5.0 %collective-permute-start.13 = (bf16[2,128,256]{2,1,0:T(8,128)(2,1)S(1)}, bf16[2,128,256]{2,1,0:T(8,128)(2,1)S(1)}, u32[]{:S(2)}, u32[]{:S(2)}) collective-permute-start(bf16[2,128,256]{2,1,0:T(8,128)(2,1)S(1)} %broadcast_select_fusion), channel_id=1, source_target_pairs={{0,26},{2,28},{4,30},{6,0},{8,2},{10,4},{12,6},{14,8},{16,10},{18,... | collective-permute-start | bytes 393224 | tf_op jit(solution)/shard_map/ppermute | solution.py:14
  39.4 1.5 collective-permute-start.9
  40.9 0.1 broadcast_select_fusion.5
  41.0 2.0 collective-permute-start.3
  43.0 0.1 broadcast_select_fusion.6
  43.1 0.1 collective-permute-start.1
  43.4 6.5 %collective-permute-done.1 = bf16[2,128,256]{2,1,0:T(8,128)(2,1)S(1)} collective-permute-done((bf16[2,128,256]{2,1,0:T(8,128)(2,1)S(1)}, bf16[2,128,256]{2,1,0:T(8,128)(2,1)S(1)}, u32[]{:S(2)}, u32[]{:S(2)}) %collective-permute-start.1) | collective-permute-done | bytes 131104 | tf_op jit(solution)/shard_map/ppermute | solution.py:14
  49.9 1.5 collective-permute-start.5
  51.6 6.0 %collective-permute-done.5 = bf16[2,128,256]{2,1,0:T(8,128)(2,1)S(1)} collective-permute-done((bf16[2,128,256]{2,1,0:T(8,128)(2,1)S(1)}, bf16[2,128,256]{2,1,0:T(8,128)(2,1)S(1)}, u32[]{:S(2)}, u32[]{:S(2)}) %collective-permute-start.5) | collective-permute-done | bytes 131104 | tf_op jit(solution)/shard_map/ppermute | solution.py:14
  57.6 2.5 %collective-permute-done.7 = bf16[2,128,256]{2,1,0:T(8,128)(2,1)S(1)} collective-permute-done((bf16[2,128,256]{2,1,0:T(8,128)(2,1)S(1)}, bf16[2,128,256]{2,1,0:T(8,128)(2,1)S(1)}, u32[]{:S(2)}, u32[]{:S(2)}) %collective-permute-start.7) | collective-permute-done | bytes 131104 | tf_op jit(solution)/shard_map/ppermute | solution.py:14
  60.1 0.1 select_dynamic-update-slice_fusion
  60.3 37.5 %while.14 = (s32[]{:T(128)}, f32[256,256]{1,0:T(8,128)S(1)}, s32[128,2]{0,1:T(2,128)S(1)}, bf16[16,128,256]{2,1,0:T(8,128)(2,1)S(1)}, bf16[128,128,128]{2,1,0:T(...) while((s32[]{:T(128)}, f32[256,256]{1,0:T(8,128)S(1)}, ...), condition=%wide.region_4.8_spmd.clone, body=%wide.region_3.7_spmd.clone.sunk | while | flops 404883648 | bytes 7349425 | solution.py:70
  60.5 0.6 gather_fusion
  61.1 1.6 gather_fusion.1
  62.7 2.3 %fusion.38 = f32[256,256]{1,0:T(8,128)S(1)} fusion(bf16[16,128,256]{2,1,0:T(8,128)(2,1)S(1)} %gather_fusion, bf16[16,128,256]{2,1,0:T(8,128)(2,1)} %gather_fusion.1, f32[16]{0:T(128)S(1)} %dynamic_slice.90, pred[16]{0:T(512)(128)(4,1)S(1)} %get-tuple-element.246, pred[16]{0:T(512)(128)(4,1)S(1)} %get-tuple-element.247, ...), kind=kOutput, calls=%fused_computation.15.clone.1 | convolution fusion | flops 404881408 | bytes 3145829 | tf_op jit(solution)/shard_map/while/body/eval_jaxpr/ar,as->rs/dot_general | solution.py:63
  65.2 0.6 gather_fusion
  65.8 1.6 gather_fusion.1
  67.4 2.3 %fusion.38 = f32[256,256]{1,0:T(8,128)S(1)} fusion(bf16[16,128,256]{2,1,0:T(8,128)(2,1)S(1)} %gather_fusion, bf16[16,128,256]{2,1,0:T(8,128)(2,1)} %gather_fusion.1, f32[16]{0:T(128)S(1)} %dynamic_slice.90, pred[16]{0:T(512)(128)(4,1)S(1)} %get-tuple-element.246, pred[16]{0:T(512)(128)(4,1)S(1)} %get-tuple-element.247, ...), kind=kOutput, calls=%fused_computation.15.clone.1 | convolution fusion | flops 404881408 | bytes 3145829 | tf_op jit(solution)/shard_map/while/body/eval_jaxpr/ar,as->rs/dot_general | solution.py:63
  69.9 0.6 gather_fusion
  70.5 1.6 gather_fusion.1
  72.1 2.3 %fusion.38 = f32[256,256]{1,0:T(8,128)S(1)} fusion(bf16[16,128,256]{2,1,0:T(8,128)(2,1)S(1)} %gather_fusion, bf16[16,128,256]{2,1,0:T(8,128)(2,1)} %gather_fusion.1, f32[16]{0:T(128)S(1)} %dynamic_slice.90, pred[16]{0:T(512)(128)(4,1)S(1)} %get-tuple-element.246, pred[16]{0:T(512)(128)(4,1)S(1)} %get-tuple-element.247, ...), kind=kOutput, calls=%fused_computation.15.clone.1 | convolution fusion | flops 404881408 | bytes 3145829 | tf_op jit(solution)/shard_map/while/body/eval_jaxpr/ar,as->rs/dot_general | solution.py:63
  74.6 0.6 gather_fusion
  75.2 1.6 gather_fusion.1
  76.8 2.3 %fusion.38 = f32[256,256]{1,0:T(8,128)S(1)} fusion(bf16[16,128,256]{2,1,0:T(8,128)(2,1)S(1)} %gather_fusion, bf16[16,128,256]{2,1,0:T(8,128)(2,1)} %gather_fusion.1, f32[16]{0:T(128)S(1)} %dynamic_slice.90, pred[16]{0:T(512)(128)(4,1)S(1)} %get-tuple-element.246, pred[16]{0:T(512)(128)(4,1)S(1)} %get-tuple-element.247, ...), kind=kOutput, calls=%fused_computation.15.clone.1 | convolution fusion | flops 404881408 | bytes 3145829 | tf_op jit(solution)/shard_map/while/body/eval_jaxpr/ar,as->rs/dot_general | solution.py:63
  79.2 0.6 gather_fusion
  79.9 1.6 gather_fusion.1
  81.5 2.3 %fusion.38 = f32[256,256]{1,0:T(8,128)S(1)} fusion(bf16[16,128,256]{2,1,0:T(8,128)(2,1)S(1)} %gather_fusion, bf16[16,128,256]{2,1,0:T(8,128)(2,1)} %gather_fusion.1, f32[16]{0:T(128)S(1)} %dynamic_slice.90, pred[16]{0:T(512)(128)(4,1)S(1)} %get-tuple-element.246, pred[16]{0:T(512)(128)(4,1)S(1)} %get-tuple-element.247, ...), kind=kOutput, calls=%fused_computation.15.clone.1 | convolution fusion | flops 404881408 | bytes 3145829 | tf_op jit(solution)/shard_map/while/body/eval_jaxpr/ar,as->rs/dot_general | solution.py:63
  83.9 0.6 gather_fusion
  84.5 1.6 gather_fusion.1
  86.2 2.3 %fusion.38 = f32[256,256]{1,0:T(8,128)S(1)} fusion(bf16[16,128,256]{2,1,0:T(8,128)(2,1)S(1)} %gather_fusion, bf16[16,128,256]{2,1,0:T(8,128)(2,1)} %gather_fusion.1, f32[16]{0:T(128)S(1)} %dynamic_slice.90, pred[16]{0:T(512)(128)(4,1)S(1)} %get-tuple-element.246, pred[16]{0:T(512)(128)(4,1)S(1)} %get-tuple-element.247, ...), kind=kOutput, calls=%fused_computation.15.clone.1 | convolution fusion | flops 404881408 | bytes 3145829 | tf_op jit(solution)/shard_map/while/body/eval_jaxpr/ar,as->rs/dot_general | solution.py:63
  88.6 0.6 gather_fusion
  89.2 1.6 gather_fusion.1
  90.8 2.3 %fusion.38 = f32[256,256]{1,0:T(8,128)S(1)} fusion(bf16[16,128,256]{2,1,0:T(8,128)(2,1)S(1)} %gather_fusion, bf16[16,128,256]{2,1,0:T(8,128)(2,1)} %gather_fusion.1, f32[16]{0:T(128)S(1)} %dynamic_slice.90, pred[16]{0:T(512)(128)(4,1)S(1)} %get-tuple-element.246, pred[16]{0:T(512)(128)(4,1)S(1)} %get-tuple-element.247, ...), kind=kOutput, calls=%fused_computation.15.clone.1 | convolution fusion | flops 404881408 | bytes 3145829 | tf_op jit(solution)/shard_map/while/body/eval_jaxpr/ar,as->rs/dot_general | solution.py:63
  93.3 0.6 gather_fusion
  93.9 1.6 gather_fusion.1
  95.5 2.3 %fusion.38 = f32[256,256]{1,0:T(8,128)S(1)} fusion(bf16[16,128,256]{2,1,0:T(8,128)(2,1)S(1)} %gather_fusion, bf16[16,128,256]{2,1,0:T(8,128)(2,1)} %gather_fusion.1, f32[16]{0:T(128)S(1)} %dynamic_slice.90, pred[16]{0:T(512)(128)(4,1)S(1)} %get-tuple-element.246, pred[16]{0:T(512)(128)(4,1)S(1)} %get-tuple-element.247, ...), kind=kOutput, calls=%fused_computation.15.clone.1 | convolution fusion | flops 404881408 | bytes 3145829 | tf_op jit(solution)/shard_map/while/body/eval_jaxpr/ar,as->rs/dot_general | solution.py:63
  97.8 0.7 copy-done.1
  98.5 104.3 %all-reduce.2.cloned.1.call-done = f32[256,256]{1,0:T(8,128)} async-done(((f32[256,256]{1,0:T(8,128)}), f32[256,256]{1,0:T(8,128)}) %all-reduce.2.cloned.1.call-update) | async-done | bytes 262160 | tf_op jit(solution)/shard_map/psum | solution.py:71
  202.9 1.7 copy.36
  (94 shorter events, 2.5 us)
Async XLA Ops:
  6.5 18.3 %copy-start = (bf16[1024,256]{1,0:T(8,128)(2,1)S(1)}, bf16[1024,256]{1,0:T(8,128)(2,1)}, u32[]{:S(2)}) copy-start(bf16[1024,256]{1,0:T(8,128)(2,1)} %param.17) | copy-start | bytes 1572868
  6.5 196.3 %all-reduce.2.cloned.1.call-start = ((), (), s32[]{:S(2)}) async-start(), calls=%async_computation | async-start | bytes 524288 | tf_op jit(solution)/shard_map/psum | solution.py:71
  10.3 15.1 %collective-permute-start.12 = (s32[2]{0:T(128)S(1)}, s32[2]{0:T(128)S(1)}, u32[]{:S(2)}, u32[]{:S(2)}) collective-permute-start(s32[2]{0:T(128)S(1)} %get-tuple-element.157), channel_id=1, source_target_pairs={{0,6},{2,8},{4,10},{6,12},{8,14},{10,16},{12,18},{14,20},{16,22},{... | collective-permute-start | bytes 32 | tf_op jit(solution)/shard_map/ppermute | solution.py:14
  14.3 11.6 %collective-permute-start.10 = (s32[2]{0:T(128)S(1)}, s32[2]{0:T(128)S(1)}, u32[]{:S(2)}, u32[]{:S(2)}) collective-permute-start(s32[2]{0:T(128)S(1)} %get-tuple-element.158), channel_id=1, source_target_pairs={{0,4},{2,6},{4,8},{6,10},{8,12},{10,14},{12,16},{14,18},{16,20},{1... | collective-permute-start | bytes 32 | tf_op jit(solution)/shard_map/ppermute | solution.py:14
  15.8 11.6 %collective-permute-start.8 = (s32[2]{0:T(128)S(1)}, s32[2]{0:T(128)S(1)}, u32[]{:S(2)}, u32[]{:S(2)}) collective-permute-start(s32[2]{0:T(128)S(1)} %get-tuple-element.159), channel_id=1, source_target_pairs={{0,2},{2,4},{4,6},{6,8},{8,10},{10,12},{12,14},{14,16},{16,18},{18... | collective-permute-start | bytes 32 | tf_op jit(solution)/shard_map/ppermute | solution.py:14
  16.4 11.0 %collective-permute-start.6 = (s32[2]{0:T(128)S(1)}, s32[2]{0:T(128)S(1)}, u32[]{:S(2)}, u32[]{:S(2)}) collective-permute-start(s32[2]{0:T(128)S(1)} %get-tuple-element.161), channel_id=1, source_target_pairs={{0,30},{2,0},{4,2},{6,4},{8,6},{10,8},{12,10},{14,12},{16,14},{18,... | collective-permute-start | bytes 32 | tf_op jit(solution)/shard_map/ppermute | solution.py:14
  21.5 6.0 %collective-permute-start.4 = (s32[2]{0:T(128)S(1)}, s32[2]{0:T(128)S(1)}, u32[]{:S(2)}, u32[]{:S(2)}) collective-permute-start(s32[2]{0:T(128)S(1)} %get-tuple-element.162), channel_id=1, source_target_pairs={{0,28},{2,30},{4,0},{6,2},{8,4},{10,6},{12,8},{14,10},{16,12},{18,... | collective-permute-start | bytes 32 | tf_op jit(solution)/shard_map/ppermute | solution.py:14
  25.5 4.5 %collective-permute-start.2 = (s32[2]{0:T(128)S(1)}, s32[2]{0:T(128)S(1)}, u32[]{:S(2)}, u32[]{:S(2)}) collective-permute-start(s32[2]{0:T(128)S(1)} %get-tuple-element.163), channel_id=1, source_target_pairs={{0,26},{2,28},{4,30},{6,0},{8,2},{10,4},{12,6},{14,8},{16,10},{18,... | collective-permute-start | bytes 32 | tf_op jit(solution)/shard_map/ppermute | solution.py:14
  25.9 4.2 %collective-permute-start = (s32[2]{0:T(128)S(1)}, s32[2]{0:T(128)S(1)}, u32[]{:S(2)}, u32[]{:S(2)}) collective-permute-start(s32[2]{0:T(128)S(1)} %get-tuple-element.164), channel_id=1, source_target_pairs={{0,24},{2,26},{4,28},{6,30},{8,0},{10,2},{12,4},{14,6},{16,8},{18,... | collective-permute-start | bytes 32 | tf_op jit(solution)/shard_map/ppermute | solution.py:14
  34.1 26.2 %collective-permute-start.13 = (bf16[2,128,256]{2,1,0:T(8,128)(2,1)S(1)}, bf16[2,128,256]{2,1,0:T(8,128)(2,1)S(1)}, u32[]{:S(2)}, u32[]{:S(2)}) collective-permute-start(bf16[2,128,256]{2,1,0:T(8,128)(2,1)S(1)} %broadcast_select_fusion), channel_id=1, source_target_pairs={{0,26},{2,28},{4,30},{6,0},{8,2},{10,4},{12,6},{14,8},{16,10},{18,... | collective-permute-start | bytes 393224 | tf_op jit(solution)/shard_map/ppermute | solution.py:14
  39.2 21.1 %collective-permute-start.11 = (bf16[2,128,256]{2,1,0:T(8,128)(2,1)S(1)}, bf16[2,128,256]{2,1,0:T(8,128)(2,1)S(1)}, u32[]{:S(2)}, u32[]{:S(2)}) collective-permute-start(bf16[2,128,256]{2,1,0:T(8,128)(2,1)S(1)} %broadcast_select_fusion.1), channel_id=1, source_target_pairs={{0,28},{2,30},{4,0},{6,2},{8,4},{10,6},{12,8},{14,10},{16,12},{18,... | collective-permute-start | bytes 393224 | tf_op jit(solution)/shard_map/ppermute | solution.py:14
  39.4 20.9 %collective-permute-start.9 = (bf16[2,128,256]{2,1,0:T(8,128)(2,1)S(1)}, bf16[2,128,256]{2,1,0:T(8,128)(2,1)S(1)}, u32[]{:S(2)}, u32[]{:S(2)}) collective-permute-start(bf16[2,128,256]{2,1,0:T(8,128)(2,1)S(1)} %broadcast_select_fusion.2), channel_id=1, source_target_pairs={{0,30},{2,0},{4,2},{6,4},{8,6},{10,8},{12,10},{14,12},{16,14},{18,... | collective-permute-start | bytes 393224 | tf_op jit(solution)/shard_map/ppermute | solution.py:14
  41.0 10.5 %collective-permute-start.3 = (bf16[2,128,256]{2,1,0:T(8,128)(2,1)S(1)}, bf16[2,128,256]{2,1,0:T(8,128)(2,1)S(1)}, u32[]{:S(2)}, u32[]{:S(2)}) collective-permute-start(bf16[2,128,256]{2,1,0:T(8,128)(2,1)S(1)} %broadcast_select_fusion.5), channel_id=1, source_target_pairs={{0,6},{2,8},{4,10},{6,12},{8,14},{10,16},{12,18},{14,20},{16,22},{... | collective-permute-start | bytes 393224 | tf_op jit(solution)/shard_map/ppermute | solution.py:14
  43.1 6.8 %collective-permute-start.1 = (bf16[2,128,256]{2,1,0:T(8,128)(2,1)S(1)}, bf16[2,128,256]{2,1,0:T(8,128)(2,1)S(1)}, u32[]{:S(2)}, u32[]{:S(2)}) collective-permute-start(bf16[2,128,256]{2,1,0:T(8,128)(2,1)S(1)} %broadcast_select_fusion.6), channel_id=1, source_target_pairs={{0,8},{2,10},{4,12},{6,14},{8,16},{10,18},{12,20},{14,22},{16,24},... | collective-permute-start | bytes 393224 | tf_op jit(solution)/shard_map/ppermute | solution.py:14
  49.9 7.7 %collective-permute-start.5 = (bf16[2,128,256]{2,1,0:T(8,128)(2,1)S(1)}, bf16[2,128,256]{2,1,0:T(8,128)(2,1)S(1)}, u32[]{:S(2)}, u32[]{:S(2)}) collective-permute-start(bf16[2,128,256]{2,1,0:T(8,128)(2,1)S(1)} %broadcast_select_fusion.4), channel_id=1, source_target_pairs={{0,4},{2,6},{4,8},{6,10},{8,12},{10,14},{12,16},{14,18},{16,20},{1... | collective-permute-start | bytes 393224 | tf_op jit(solution)/shard_map/ppermute | solution.py:14
  51.5 8.6 %collective-permute-start.7 = (bf16[2,128,256]{2,1,0:T(8,128)(2,1)S(1)}, bf16[2,128,256]{2,1,0:T(8,128)(2,1)S(1)}, u32[]{:S(2)}, u32[]{:S(2)}) collective-permute-start(bf16[2,128,256]{2,1,0:T(8,128)(2,1)S(1)} %broadcast_select_fusion.3), channel_id=1, source_target_pairs={{0,2},{2,4},{4,6},{6,8},{8,10},{10,12},{12,14},{14,16},{16,18},{18... | collective-permute-start | bytes 393224 | tf_op jit(solution)/shard_map/ppermute | solution.py:14
  97.8 0.7 copy-start.1
Sparse Core Ops, SparseCore 0:
  98.6 104.1 all-reduce.1
where the time goes:
time: 212 us; the launch traced here: 211 us
  waiting for transfers between devices  122 us (58%)
  local copies, waits for them, and re-layouts  31.4 us (15%)
  starting transfers between devices  23.9 us (11%)
  matrix products  18 us (8%)
  between operations  14.5 us (7%)
    psum x1, waiting for transfers between devices, on_device(): reduced = lax.psum(partial_sum, 'dom')  104 us
    ppermute x14, starting transfers between devices, shifted(): return lax.ppermute(value, axis, pairs)  23.9 us
    dot_general x8, matrix products, project(): jnp.einsum('ar,as->rs', rows.reshape(GROUP * block, rank), right.reshape(...  18 us
    ppermute x14, waiting for transfers between devices, shifted(): return lax.ppermute(value, axis, pairs)  17.6 us
    gather x8, local copies, waits for them, and re-layouts, project(): rows = jnp.take(fetched, link_set[:, 0], axis=0)  12.8 us
    gather x8, local copies, waits for them, and re-layouts, project(): cols = jnp.take(fetched, link_set[:, 1], axis=0)  4.91 us
  transfers between devices with their start and end apart: 15, of which 5 were waited for; matrix products, arithmetic and copies ran while one was open for 2% of the time, Pallas kernels for 0%

commit v1 on v0

--- a/solution.py
+++ b/solution.py
@@ -68,7 +68,8 @@
         )
 
     partial_sum = lax.fori_loop(0, tile_dev // GROUP, project, jnp.zeros((rank, rank), jnp.float32))
-    reduced = lax.psum(partial_sum, "dom")
+    parts = lax.all_gather(partial_sum, "dom", axis=0, tiled=False)
+    reduced = parts.sum(axis=0)
     return reduced
 
 

time: 212 us -> 181 us (0.85)
  waiting for transfers between devices: 122 us -> 89.6 us
  other arithmetic: 1.3 us -> 4.48 us
    psum x1 -> x0, waiting for transfers between devices: 104 us -> none  [on_device(): reduced = lax.psum(partial_sum, 'dom')]
    all_gather x0 -> x1, waiting for transfers between devices: none -> 72.1 us  [on_device(): parts = lax.all_gather(partial_sum, 'dom', axis=0, tiled=False)]
    reduce_sum x0 -> x1, other arithmetic: none -> 3.18 us  [on_device(): reduced = parts.sum(axis=0)]
where the time goes in v1:
time: 181 us
  waiting for transfers between devices  89.6 us (50%)
  local copies, waits for them, and re-layouts  29.7 us (16%)
  starting transfers between devices  23.9 us (13%)
  matrix products  18 us (10%)
  between operations  14.5 us (8%)
  other arithmetic  4.48 us (2%)
    all_gather x1, waiting for transfers between devices, on_device(): parts = lax.all_gather(partial_sum, 'dom', axis=0, tiled=False)  72.1 us
    ppermute x14, starting transfers between devices, shifted(): return lax.ppermute(value, axis, pairs)  23.9 us
    dot_general x8, matrix products, project(): jnp.einsum('ar,as->rs', rows.reshape(GROUP * block, rank), right.reshape(...  18 us
    ppermute x14, waiting for transfers between devices, shifted(): return lax.ppermute(value, axis, pairs)  17.6 us
    gather x8, local copies, waits for them, and re-layouts, project(): rows = jnp.take(fetched, link_set[:, 0], axis=0)  12.8 us
    gather x8, local copies, waits for them, and re-layouts, project(): cols = jnp.take(fetched, link_set[:, 1], axis=0)  4.91 us
    gather x7, local copies, waits for them, and re-layouts, on_device(): served = jnp.take(stored, asked, axis=0)  3.89 us
  transfers between devices with their start and end apart: 15, of which 5 were waited for; matrix products, arithmetic and copies ran while one was open for 2% of the time, Pallas kernels for 0%

profile of v1, /device:TPU:0, one launch (start us, length us, event | category | flops | bytes accessed | tf_op | source)
XLA Modules:
  0.0 180.6 jit_solution(5840417314438624343)
XLA Ops:
  6.5 0.8 copy.16
  7.4 0.1 reshape.52
  7.5 1.9 %gather_fusion.2 = s32[256]{0:T(256)S(1)} fusion(s32[128]{0:T(128)} %param.15, s32[1024]{0:T(1024)S(1)} %pad_clamp_fusion.11), kind=kCustom, calls=%fused_computation.clone | custom fusion | bytes 3072 | tf_op jit(solution)/shard_map/jit(_take)/gather | solution.py:24
  9.5 0.1 fusion.18
  9.7 0.2 reduce_window_sum.11
  10.0 0.3 fusion.29
  10.3 4.0 %collective-permute-start.12 = (s32[2]{0:T(128)S(1)}, s32[2]{0:T(128)S(1)}, u32[]{:S(2)}, u32[]{:S(2)}) collective-permute-start(s32[2]{0:T(128)S(1)} %get-tuple-element.157), channel_id=1, source_target_pairs={{0,6},{2,8},{4,10},{6,12},{8,14},{10,16},{12,18},{14,20},{16,22},{... | collective-permute-start | bytes 32 | tf_op jit(solution)/shard_map/ppermute | solution.py:14
  14.3 1.5 collective-permute-start.10
  15.8 0.6 collective-permute-start.8
  16.4 5.0 %collective-permute-start.6 = (s32[2]{0:T(128)S(1)}, s32[2]{0:T(128)S(1)}, u32[]{:S(2)}, u32[]{:S(2)}) collective-permute-start(s32[2]{0:T(128)S(1)} %get-tuple-element.161), channel_id=1, source_target_pairs={{0,30},{2,0},{4,2},{6,4},{8,6},{10,8},{12,10},{14,12},{16,14},{18,... | collective-permute-start | bytes 32 | tf_op jit(solution)/shard_map/ppermute | solution.py:14
  21.5 0.5 collective-permute-start.4
  22.0 0.1 sub.22
  22.8 1.9 %gather_fusion.3 = s32[256]{0:T(256)S(1)} fusion(s32[128]{0:T(128)S(1)} %sub.22, s32[1024]{0:T(1024)S(1)} %pad_clamp_fusion.10), kind=kCustom, calls=%fused_computation.3.clone | custom fusion | bytes 3072 | tf_op jit(solution)/shard_map/jit(_take)/gather | solution.py:35
  24.7 0.1 reshape.53
  24.9 0.6 gather_fusion.8
  25.5 0.4 collective-permute-start.2
  25.9 1.5 collective-permute-start
  27.5 2.5 %collective-permute-done.2 = s32[2]{0:T(128)S(1)} collective-permute-done((s32[2]{0:T(128)S(1)}, s32[2]{0:T(128)S(1)}, u32[]{:S(2)}, u32[]{:S(2)}) %collective-permute-start.2) | collective-permute-done | bytes 40 | tf_op jit(solution)/shard_map/ppermute | solution.py:14
  30.0 0.6 gather_fusion.4
  30.6 0.6 gather_fusion.5
  31.2 0.6 gather_fusion.6
  31.7 0.6 gather_fusion.7
  32.3 0.6 gather_fusion.9
  32.9 0.6 gather_fusion.10
  33.4 0.6 gather_fusion.11
  34.1 5.0 %collective-permute-start.13 = (bf16[2,128,256]{2,1,0:T(8,128)(2,1)S(1)}, bf16[2,128,256]{2,1,0:T(8,128)(2,1)S(1)}, u32[]{:S(2)}, u32[]{:S(2)}) collective-permute-start(bf16[2,128,256]{2,1,0:T(8,128)(2,1)S(1)} %broadcast_select_fusion), channel_id=1, source_target_pairs={{0,26},{2,28},{4,30},{6,0},{8,2},{10,4},{12,6},{14,8},{16,10},{18,... | collective-permute-start | bytes 393224 | tf_op jit(solution)/shard_map/ppermute | solution.py:14
  39.4 1.5 collective-permute-start.9
  40.9 0.1 broadcast_select_fusion.5
  41.0 2.0 %collective-permute-start.3 = (bf16[2,128,256]{2,1,0:T(8,128)(2,1)S(1)}, bf16[2,128,256]{2,1,0:T(8,128)(2,1)S(1)}, u32[]{:S(2)}, u32[]{:S(2)}) collective-permute-start(bf16[2,128,256]{2,1,0:T(8,128)(2,1)S(1)} %broadcast_select_fusion.5), channel_id=1, source_target_pairs={{0,6},{2,8},{4,10},{6,12},{8,14},{10,16},{12,18},{14,20},{16,22},{... | collective-permute-start | bytes 393224 | tf_op jit(solution)/shard_map/ppermute | solution.py:14
  43.0 0.1 broadcast_select_fusion.6
  43.1 0.1 collective-permute-start.1
  43.4 6.5 %collective-permute-done.1 = bf16[2,128,256]{2,1,0:T(8,128)(2,1)S(1)} collective-permute-done((bf16[2,128,256]{2,1,0:T(8,128)(2,1)S(1)}, bf16[2,128,256]{2,1,0:T(8,128)(2,1)S(1)}, u32[]{:S(2)}, u32[]{:S(2)}) %collective-permute-start.1) | collective-permute-done | bytes 131104 | tf_op jit(solution)/shard_map/ppermute | solution.py:14
  49.9 1.5 collective-permute-start.5
  51.6 6.0 %collective-permute-done.5 = bf16[2,128,256]{2,1,0:T(8,128)(2,1)S(1)} collective-permute-done((bf16[2,128,256]{2,1,0:T(8,128)(2,1)S(1)}, bf16[2,128,256]{2,1,0:T(8,128)(2,1)S(1)}, u32[]{:S(2)}, u32[]{:S(2)}) %collective-permute-start.5) | collective-permute-done | bytes 131104 | tf_op jit(solution)/shard_map/ppermute | solution.py:14
  57.6 2.5 %collective-permute-done.7 = bf16[2,128,256]{2,1,0:T(8,128)(2,1)S(1)} collective-permute-done((bf16[2,128,256]{2,1,0:T(8,128)(2,1)S(1)}, bf16[2,128,256]{2,1,0:T(8,128)(2,1)S(1)}, u32[]{:S(2)}, u32[]{:S(2)}) %collective-permute-start.7) | collective-permute-done | bytes 131104 | tf_op jit(solution)/shard_map/ppermute | solution.py:14
  60.1 0.1 select_dynamic-update-slice_fusion
  60.3 37.5 %while.14 = (s32[]{:T(128)}, f32[256,256]{1,0:T(8,128)S(1)}, s32[128,2]{0,1:T(2,128)S(1)}, bf16[16,128,256]{2,1,0:T(8,128)(2,1)S(1)}, bf16[128,128,128]{2,1,0:T(...) while((s32[]{:T(128)}, f32[256,256]{1,0:T(8,128)S(1)}, ...), condition=%wide.region_4.8_spmd.clone, body=%wide.region_3.7_spmd.clone.sunk | while | flops 404883648 | bytes 7349425 | solution.py:70
  60.5 0.6 gather_fusion
  61.1 1.6 gather_fusion.1
  62.7 2.3 %fusion.38 = f32[256,256]{1,0:T(8,128)S(1)} fusion(bf16[16,128,256]{2,1,0:T(8,128)(2,1)S(1)} %gather_fusion, bf16[16,128,256]{2,1,0:T(8,128)(2,1)} %gather_fusion.1, f32[16]{0:T(128)S(1)} %dynamic_slice.90, pred[16]{0:T(512)(128)(4,1)S(1)} %get-tuple-element.246, pred[16]{0:T(512)(128)(4,1)S(1)} %get-tuple-element.247, ...), kind=kOutput, calls=%fused_computation.15.clone.1 | convolution fusion | flops 404881408 | bytes 3145829 | tf_op jit(solution)/shard_map/while/body/eval_jaxpr/ar,as->rs/dot_general | solution.py:63
  65.2 0.6 gather_fusion
  65.8 1.6 gather_fusion.1
  67.4 2.3 %fusion.38 = f32[256,256]{1,0:T(8,128)S(1)} fusion(bf16[16,128,256]{2,1,0:T(8,128)(2,1)S(1)} %gather_fusion, bf16[16,128,256]{2,1,0:T(8,128)(2,1)} %gather_fusion.1, f32[16]{0:T(128)S(1)} %dynamic_slice.90, pred[16]{0:T(512)(128)(4,1)S(1)} %get-tuple-element.246, pred[16]{0:T(512)(128)(4,1)S(1)} %get-tuple-element.247, ...), kind=kOutput, calls=%fused_computation.15.clone.1 | convolution fusion | flops 404881408 | bytes 3145829 | tf_op jit(solution)/shard_map/while/body/eval_jaxpr/ar,as->rs/dot_general | solution.py:63
  69.9 0.6 gather_fusion
  70.5 1.6 gather_fusion.1
  72.1 2.3 %fusion.38 = f32[256,256]{1,0:T(8,128)S(1)} fusion(bf16[16,128,256]{2,1,0:T(8,128)(2,1)S(1)} %gather_fusion, bf16[16,128,256]{2,1,0:T(8,128)(2,1)} %gather_fusion.1, f32[16]{0:T(128)S(1)} %dynamic_slice.90, pred[16]{0:T(512)(128)(4,1)S(1)} %get-tuple-element.246, pred[16]{0:T(512)(128)(4,1)S(1)} %get-tuple-element.247, ...), kind=kOutput, calls=%fused_computation.15.clone.1 | convolution fusion | flops 404881408 | bytes 3145829 | tf_op jit(solution)/shard_map/while/body/eval_jaxpr/ar,as->rs/dot_general | solution.py:63
  74.6 0.6 gather_fusion
  75.2 1.6 gather_fusion.1
  76.8 2.3 %fusion.38 = f32[256,256]{1,0:T(8,128)S(1)} fusion(bf16[16,128,256]{2,1,0:T(8,128)(2,1)S(1)} %gather_fusion, bf16[16,128,256]{2,1,0:T(8,128)(2,1)} %gather_fusion.1, f32[16]{0:T(128)S(1)} %dynamic_slice.90, pred[16]{0:T(512)(128)(4,1)S(1)} %get-tuple-element.246, pred[16]{0:T(512)(128)(4,1)S(1)} %get-tuple-element.247, ...), kind=kOutput, calls=%fused_computation.15.clone.1 | convolution fusion | flops 404881408 | bytes 3145829 | tf_op jit(solution)/shard_map/while/body/eval_jaxpr/ar,as->rs/dot_general | solution.py:63
  79.2 0.6 gather_fusion
  79.9 1.6 gather_fusion.1
  81.5 2.3 %fusion.38 = f32[256,256]{1,0:T(8,128)S(1)} fusion(bf16[16,128,256]{2,1,0:T(8,128)(2,1)S(1)} %gather_fusion, bf16[16,128,256]{2,1,0:T(8,128)(2,1)} %gather_fusion.1, f32[16]{0:T(128)S(1)} %dynamic_slice.90, pred[16]{0:T(512)(128)(4,1)S(1)} %get-tuple-element.246, pred[16]{0:T(512)(128)(4,1)S(1)} %get-tuple-element.247, ...), kind=kOutput, calls=%fused_computation.15.clone.1 | convolution fusion | flops 404881408 | bytes 3145829 | tf_op jit(solution)/shard_map/while/body/eval_jaxpr/ar,as->rs/dot_general | solution.py:63
  83.9 0.6 gather_fusion
  84.5 1.6 gather_fusion.1
  86.2 2.3 %fusion.38 = f32[256,256]{1,0:T(8,128)S(1)} fusion(bf16[16,128,256]{2,1,0:T(8,128)(2,1)S(1)} %gather_fusion, bf16[16,128,256]{2,1,0:T(8,128)(2,1)} %gather_fusion.1, f32[16]{0:T(128)S(1)} %dynamic_slice.90, pred[16]{0:T(512)(128)(4,1)S(1)} %get-tuple-element.246, pred[16]{0:T(512)(128)(4,1)S(1)} %get-tuple-element.247, ...), kind=kOutput, calls=%fused_computation.15.clone.1 | convolution fusion | flops 404881408 | bytes 3145829 | tf_op jit(solution)/shard_map/while/body/eval_jaxpr/ar,as->rs/dot_general | solution.py:63
  88.6 0.6 gather_fusion
  89.2 1.6 gather_fusion.1
  90.8 2.3 %fusion.38 = f32[256,256]{1,0:T(8,128)S(1)} fusion(bf16[16,128,256]{2,1,0:T(8,128)(2,1)S(1)} %gather_fusion, bf16[16,128,256]{2,1,0:T(8,128)(2,1)} %gather_fusion.1, f32[16]{0:T(128)S(1)} %dynamic_slice.90, pred[16]{0:T(512)(128)(4,1)S(1)} %get-tuple-element.246, pred[16]{0:T(512)(128)(4,1)S(1)} %get-tuple-element.247, ...), kind=kOutput, calls=%fused_computation.15.clone.1 | convolution fusion | flops 404881408 | bytes 3145829 | tf_op jit(solution)/shard_map/while/body/eval_jaxpr/ar,as->rs/dot_general | solution.py:63
  93.3 0.6 gather_fusion
  93.9 1.6 gather_fusion.1
  95.5 2.3 %fusion.38 = f32[256,256]{1,0:T(8,128)S(1)} fusion(bf16[16,128,256]{2,1,0:T(8,128)(2,1)S(1)} %gather_fusion, bf16[16,128,256]{2,1,0:T(8,128)(2,1)} %gather_fusion.1, f32[16]{0:T(128)S(1)} %dynamic_slice.90, pred[16]{0:T(512)(128)(4,1)S(1)} %get-tuple-element.246, pred[16]{0:T(512)(128)(4,1)S(1)} %get-tuple-element.247, ...), kind=kOutput, calls=%fused_computation.15.clone.1 | convolution fusion | flops 404881408 | bytes 3145829 | tf_op jit(solution)/shard_map/while/body/eval_jaxpr/ar,as->rs/dot_general | solution.py:63
  97.8 0.7 copy-done.1
  98.5 72.1 %all-gather.3.cloned.1.call-done = f32[4096,256]{1,0:T(8,128)} async-done(((f32[256,256]{1,0:T(8,128)}), f32[4096,256]{1,0:T(8,128)}) %all-gather.3.cloned.1.call-update) | async-done | bytes 4194320 | tf_op jit(solution)/shard_map/all_gather | solution.py:71
  170.6 3.2 %reduce_sum.19 = f32[256,256]{1,0:T(8,128)} reduce(f32[16,256,256]{2,1,0:T(8,128)} %bitcast.24, f32[]{:T(128)} %constant.157.clone.1), dimensions={0}, to_apply=%region_5.9 | reduce | flops 983040 | bytes 4456452 | tf_op jit(solution)/shard_map/reduce_sum | solution.py:72
  (94 shorter events, 2.5 us)
Async XLA Ops:
  6.5 18.3 %copy-start = (bf16[1024,256]{1,0:T(8,128)(2,1)S(1)}, bf16[1024,256]{1,0:T(8,128)(2,1)}, u32[]{:S(2)}) copy-start(bf16[1024,256]{1,0:T(8,128)(2,1)} %param.17) | copy-start | bytes 1572868
  6.5 164.0 %all-gather.3.cloned.1.call-start = ((), (), s32[]{:S(2)}) async-start(), calls=%async_computation | async-start | bytes 4456448 | tf_op jit(solution)/shard_map/all_gather | solution.py:71
  10.3 15.1 %collective-permute-start.12 = (s32[2]{0:T(128)S(1)}, s32[2]{0:T(128)S(1)}, u32[]{:S(2)}, u32[]{:S(2)}) collective-permute-start(s32[2]{0:T(128)S(1)} %get-tuple-element.157), channel_id=1, source_target_pairs={{0,6},{2,8},{4,10},{6,12},{8,14},{10,16},{12,18},{14,20},{16,22},{... | collective-permute-start | bytes 32 | tf_op jit(solution)/shard_map/ppermute | solution.py:14
  14.3 11.6 %collective-permute-start.10 = (s32[2]{0:T(128)S(1)}, s32[2]{0:T(128)S(1)}, u32[]{:S(2)}, u32[]{:S(2)}) collective-permute-start(s32[2]{0:T(128)S(1)} %get-tuple-element.158), channel_id=1, source_target_pairs={{0,4},{2,6},{4,8},{6,10},{8,12},{10,14},{12,16},{14,18},{16,20},{1... | collective-permute-start | bytes 32 | tf_op jit(solution)/shard_map/ppermute | solution.py:14
  15.8 11.6 %collective-permute-start.8 = (s32[2]{0:T(128)S(1)}, s32[2]{0:T(128)S(1)}, u32[]{:S(2)}, u32[]{:S(2)}) collective-permute-start(s32[2]{0:T(128)S(1)} %get-tuple-element.159), channel_id=1, source_target_pairs={{0,2},{2,4},{4,6},{6,8},{8,10},{10,12},{12,14},{14,16},{16,18},{18... | collective-permute-start | bytes 32 | tf_op jit(solution)/shard_map/ppermute | solution.py:14
  16.4 11.0 %collective-permute-start.6 = (s32[2]{0:T(128)S(1)}, s32[2]{0:T(128)S(1)}, u32[]{:S(2)}, u32[]{:S(2)}) collective-permute-start(s32[2]{0:T(128)S(1)} %get-tuple-element.161), channel_id=1, source_target_pairs={{0,30},{2,0},{4,2},{6,4},{8,6},{10,8},{12,10},{14,12},{16,14},{18,... | collective-permute-start | bytes 32 | tf_op jit(solution)/shard_map/ppermute | solution.py:14
  21.5 6.0 %collective-permute-start.4 = (s32[2]{0:T(128)S(1)}, s32[2]{0:T(128)S(1)}, u32[]{:S(2)}, u32[]{:S(2)}) collective-permute-start(s32[2]{0:T(128)S(1)} %get-tuple-element.162), channel_id=1, source_target_pairs={{0,28},{2,30},{4,0},{6,2},{8,4},{10,6},{12,8},{14,10},{16,12},{18,... | collective-permute-start | bytes 32 | tf_op jit(solution)/shard_map/ppermute | solution.py:14
  25.5 4.5 %collective-permute-start.2 = (s32[2]{0:T(128)S(1)}, s32[2]{0:T(128)S(1)}, u32[]{:S(2)}, u32[]{:S(2)}) collective-permute-start(s32[2]{0:T(128)S(1)} %get-tuple-element.163), channel_id=1, source_target_pairs={{0,26},{2,28},{4,30},{6,0},{8,2},{10,4},{12,6},{14,8},{16,10},{18,... | collective-permute-start | bytes 32 | tf_op jit(solution)/shard_map/ppermute | solution.py:14
  25.9 4.2 %collective-permute-start = (s32[2]{0:T(128)S(1)}, s32[2]{0:T(128)S(1)}, u32[]{:S(2)}, u32[]{:S(2)}) collective-permute-start(s32[2]{0:T(128)S(1)} %get-tuple-element.164), channel_id=1, source_target_pairs={{0,24},{2,26},{4,28},{6,30},{8,0},{10,2},{12,4},{14,6},{16,8},{18,... | collective-permute-start | bytes 32 | tf_op jit(solution)/shard_map/ppermute | solution.py:14
  34.1 26.2 %collective-permute-start.13 = (bf16[2,128,256]{2,1,0:T(8,128)(2,1)S(1)}, bf16[2,128,256]{2,1,0:T(8,128)(2,1)S(1)}, u32[]{:S(2)}, u32[]{:S(2)}) collective-permute-start(bf16[2,128,256]{2,1,0:T(8,128)(2,1)S(1)} %broadcast_select_fusion), channel_id=1, source_target_pairs={{0,26},{2,28},{4,30},{6,0},{8,2},{10,4},{12,6},{14,8},{16,10},{18,... | collective-permute-start | bytes 393224 | tf_op jit(solution)/shard_map/ppermute | solution.py:14
  39.2 21.1 %collective-permute-start.11 = (bf16[2,128,256]{2,1,0:T(8,128)(2,1)S(1)}, bf16[2,128,256]{2,1,0:T(8,128)(2,1)S(1)}, u32[]{:S(2)}, u32[]{:S(2)}) collective-permute-start(bf16[2,128,256]{2,1,0:T(8,128)(2,1)S(1)} %broadcast_select_fusion.1), channel_id=1, source_target_pairs={{0,28},{2,30},{4,0},{6,2},{8,4},{10,6},{12,8},{14,10},{16,12},{18,... | collective-permute-start | bytes 393224 | tf_op jit(solution)/shard_map/ppermute | solution.py:14
  39.4 20.9 %collective-permute-start.9 = (bf16[2,128,256]{2,1,0:T(8,128)(2,1)S(1)}, bf16[2,128,256]{2,1,0:T(8,128)(2,1)S(1)}, u32[]{:S(2)}, u32[]{:S(2)}) collective-permute-start(bf16[2,128,256]{2,1,0:T(8,128)(2,1)S(1)} %broadcast_select_fusion.2), channel_id=1, source_target_pairs={{0,30},{2,0},{4,2},{6,4},{8,6},{10,8},{12,10},{14,12},{16,14},{18,... | collective-permute-start | bytes 393224 | tf_op jit(solution)/shard_map/ppermute | solution.py:14
  41.0 10.5 %collective-permute-start.3 = (bf16[2,128,256]{2,1,0:T(8,128)(2,1)S(1)}, bf16[2,128,256]{2,1,0:T(8,128)(2,1)S(1)}, u32[]{:S(2)}, u32[]{:S(2)}) collective-permute-start(bf16[2,128,256]{2,1,0:T(8,128)(2,1)S(1)} %broadcast_select_fusion.5), channel_id=1, source_target_pairs={{0,6},{2,8},{4,10},{6,12},{8,14},{10,16},{12,18},{14,20},{16,22},{... | collective-permute-start | bytes 393224 | tf_op jit(solution)/shard_map/ppermute | solution.py:14
  43.1 6.8 %collective-permute-start.1 = (bf16[2,128,256]{2,1,0:T(8,128)(2,1)S(1)}, bf16[2,128,256]{2,1,0:T(8,128)(2,1)S(1)}, u32[]{:S(2)}, u32[]{:S(2)}) collective-permute-start(bf16[2,128,256]{2,1,0:T(8,128)(2,1)S(1)} %broadcast_select_fusion.6), channel_id=1, source_target_pairs={{0,8},{2,10},{4,12},{6,14},{8,16},{10,18},{12,20},{14,22},{16,24},... | collective-permute-start | bytes 393224 | tf_op jit(solution)/shard_map/ppermute | solution.py:14
  49.9 7.7 %collective-permute-start.5 = (bf16[2,128,256]{2,1,0:T(8,128)(2,1)S(1)}, bf16[2,128,256]{2,1,0:T(8,128)(2,1)S(1)}, u32[]{:S(2)}, u32[]{:S(2)}) collective-permute-start(bf16[2,128,256]{2,1,0:T(8,128)(2,1)S(1)} %broadcast_select_fusion.4), channel_id=1, source_target_pairs={{0,4},{2,6},{4,8},{6,10},{8,12},{10,14},{12,16},{14,18},{16,20},{1... | collective-permute-start | bytes 393224 | tf_op jit(solution)/shard_map/ppermute | solution.py:14
  51.5 8.6 %collective-permute-start.7 = (bf16[2,128,256]{2,1,0:T(8,128)(2,1)S(1)}, bf16[2,128,256]{2,1,0:T(8,128)(2,1)S(1)}, u32[]{:S(2)}, u32[]{:S(2)}) collective-permute-start(bf16[2,128,256]{2,1,0:T(8,128)(2,1)S(1)} %broadcast_select_fusion.3), channel_id=1, source_target_pairs={{0,2},{2,4},{4,6},{6,8},{8,10},{10,12},{12,14},{14,16},{16,18},{18... | collective-permute-start | bytes 393224 | tf_op jit(solution)/shard_map/ppermute | solution.py:14
  97.8 0.7 copy-start.1
Sparse Core Ops, SparseCore 0:
  98.6 71.8 all-gather.2
